TPU v7x, 16 devices: a 4x2x1 block of a 4x4x8 slice. The times are simulated.
16 devices in a mesh: dp: 2 (over y, z), tp: 8 (over x, core).
Axes of the slice: x: 4, y: 2, z: 1, core: 2. Of those that a mesh axis runs over, the one named last changes fastest.
The devices are a block of a 4x4x8 slice.
Arguments:
- tokens: int32 [2, 128], P('dp'), parts along dimension 0
- positions: int32 [2, 128], P('dp'), parts along dimension 0
- embedding: bfloat16 [16384, 3072], P('tp')
- gain_attn: float32 [3072], replicated
- gain_mlp: float32 [3072], replicated
- w_query: bfloat16 [3072, 24, 128], P(None, 'tp')
- w_key: bfloat16 [3072, 8, 128], P(None, 'tp')
- w_value: bfloat16 [3072, 8, 128], P(None, 'tp')
- w_out: bfloat16 [24, 128, 3072], P('tp')
- w_gate: bfloat16 [3072, 8192], P(None, 'tp')
- w_up: bfloat16 [3072, 8192], P(None, 'tp')
- w_down: bfloat16 [8192, 3072], P('tp')
- grad_hidden: bfloat16 [2, 128, 3072], P('dp', 'tp'), parts along dimension 0
Outputs:
- output 1: bfloat16 [2, 128, 3072], P('dp', 'tp'), parts along dimension 0
- output 2: float32 [32768, 3072], P(('dp', 'tp')), parts along dimension 0
- output 3: float32 [6144, 24, 128], P('dp', 'tp'), parts along dimension 0
- output 4: float32 [6144, 8, 128], P('dp', 'tp'), parts along dimension 0
- output 5: float32 [6144, 8, 128], P('dp', 'tp'), parts along dimension 0
- output 6: float32 [48, 128, 3072], P(('dp', 'tp')), parts along dimension 0
- output 7: float32 [6144, 8192], P('dp', 'tp'), parts along dimension 0
- output 8: float32 [6144, 8192], P('dp', 'tp'), parts along dimension 0
- output 9: float32 [16384, 3072], P(('dp', 'tp')), parts along dimension 0
- output 10: float32 [6144], P('dp'), parts along dimension 0
- output 11: float32 [6144], P('dp'), parts along dimension 0
There are 2 independent parts. A program takes and returns all parts, laid end to end along the dimension named above; an argument that names none is the same for every part.
All inputs are finite; a program needn't handle non-finite values.
Results may differ from a plain program's by a relative error of at most 0.02.
Values are sent between devices in bfloat16 or wider.
A program may use at most 768 MiB of HBM per device.

v0:
```python
import functools

import jax
import jax.numpy as jnp
from jax import lax
from jax.experimental import pallas as pl
from jax.experimental.pallas import tpu as pltpu
from jax.sharding import PartitionSpec as P

ROPE_THETA = 1000000.0
RMS_EPS = 1e-5
BF = jnp.bfloat16
F32 = jnp.float32
VMEM_FULL = 67043328
CHIPS = 4
CORES = 2


def dot(a, b):
    return lax.dot_general(a, b, (((1,), (0,)), ((), ())), preferred_element_type=F32)


def dot_bt(a, b):
    return lax.dot_general(a, b, (((1,), (1,)), ((), ())), preferred_element_type=F32)


def dot_at(a, b):
    return lax.dot_general(a, b, (((0,), (0,)), ((), ())), preferred_element_type=F32)


class Place:
    def __init__(self):
        me = lax.axis_index('tp')
        self.chip, self.core = me // CORES, me % CORES
        self.right_chip = (self.chip + 1) % CHIPS
        self.left_chip = (self.chip + CHIPS - 1) % CHIPS
        self.far_chip = (self.chip + 2) % CHIPS
        self.me = me
        self.other = 1 - self.core
        self.partner = self.chip * CORES + self.other
        self.right = self.right_chip * CORES + self.core
        self.left = self.left_chip * CORES + self.core
        self.far = self.far_chip * CORES + self.core


def remote(src, dst, send, recv, device):
    return pltpu.make_async_remote_copy(src_ref=src, dst_ref=dst, send_sem=send, recv_sem=recv,
                                        device_id={'tp': device}, device_id_type=pl.DeviceIdType.MESH)


def entry_barrier(pos):
    barrier = pltpu.get_barrier_semaphore()
    for device in (pos.left, pos.right, pos.partner):
        pl.semaphore_signal(barrier, inc=1, device_id={'tp': device}, device_id_type=pl.DeviceIdType.MESH)
    pl.semaphore_wait(barrier, 3)


class Gather:
    def __init__(self, pos, buf, send, recv):
        self.pos, self.buf = pos, buf
        half = buf.shape[-1] // 2
        p = pos
        other = p.other - p.core

        def piece(slot, part):
            if part == 2:
                return buf.at[slot]
            return buf.at[slot, :, pl.ds(part * half, half)]

        def copy(index, slot, part, device):
            ref = piece(slot, part)
            return remote(ref, ref, send.at[index], recv.at[index], device)

        plan = {
            0: ((p.me, 0, p.right), (p.left, 0)), 1: ((p.me, 1, p.left), (p.right, 1)),
            2: ((p.me, 2, p.partner), (p.partner, 2)),
            3: ((p.me, 1, p.right), (p.left, 1)), 4: ((p.me, 0, p.left), (p.right, 0)),
            5: ((p.left, 0, p.right), (p.far, 0)), 6: ((p.right, 1, p.left), (p.far, 1)),
            7: ((p.left, 0, p.partner), (p.left + other, 0)), 8: ((p.right, 1, p.partner), (p.right + other, 1)),
            9: ((p.left, 1, p.partner), (p.left + other, 1)), 10: ((p.right, 0, p.partner), (p.right + other, 0)),
            11: ((p.far, 0, p.partner), (p.far + other, 0)), 12: ((p.far, 1, p.partner), (p.far + other, 1)),
        }
        self.out = {i: copy(i, *s) for i, (s, _) in plan.items()}
        self.into = {i: copy(i, slot, part, p.partner) for i, (_, (slot, part)) in plan.items()}

    def start(self):
        for i in (0, 1, 2, 3, 4):
            self.out[i].start()

    def relay(self):
        for i, onward in ((0, (5, 7)), (1, (6, 8)), (3, (9,)), (4, (10,))):
            self.into[i].wait_recv()
            for j in onward:
                self.out[j].start()

    def finish(self):
        for i, j in ((5, 11), (6, 12)):
            self.into[i].wait_recv()
            self.out[j].start()
        for i in (2, 7, 8, 9, 10, 11, 12):
            self.into[i].wait_recv()

    def drain(self):
        for i in range(13):
            self.out[i].wait_send()

    def run(self):
        self.start()
        self.relay()
        self.finish()
        self.drain()


class Scatter:
    def __init__(self, pos, part, from_partner, work, arrive, send, recv):
        p = pos
        self.pos, self.part, self.from_partner, self.work, self.arrive = p, part, from_partner, work, arrive
        self.half = work.shape[-1]
        self.chips = (p.far_chip, p.right_chip, p.left_chip, p.chip)
        self.inner = [remote(part.at[p.other, y], from_partner.at[y], send.at[k], recv.at[k], p.partner)
                      for k, y in enumerate(self.chips)]
        self.outer = [remote(work.at[k], arrive.at[k], send.at[4 + k], recv.at[4 + k], p.right if k % 2 == 0 else p.left)
                      for k in range(6)]

    def pair(self, k, part):
        cols = pl.ds(part * self.half, self.half)
        y = self.chips[k]
        return self.part[self.pos.core, y, :, cols].astype(F32) + self.from_partner[y, :, cols].astype(F32)

    def send_sum(self, k, value):
        self.work[k] = value.astype(BF)
        self.outer[k].start()

    def start(self):
        for copy in self.inner:
            copy.start()

    def relay(self):
        self.inner[0].wait_recv()
        self.send_sum(0, self.pair(0, 0))
        self.send_sum(1, self.pair(0, 1))
        self.inner[1].wait_recv()
        self.send_sum(2, self.pair(1, 1))
        self.inner[2].wait_recv()
        self.send_sum(3, self.pair(2, 0))
        self.outer[0].wait_recv()
        self.send_sum(4, self.pair(1, 0) + self.arrive[0].astype(F32))
        self.outer[1].wait_recv()
        self.send_sum(5, self.pair(2, 1) + self.arrive[1].astype(F32))

    def finish(self):
        self.inner[3].wait_recv()
        for k in (2, 3, 4, 5):
            self.outer[k].wait_recv()
        low = self.pair(3, 0) + self.arrive[3].astype(F32) + self.arrive[4].astype(F32)
        high = self.pair(3, 1) + self.arrive[2].astype(F32) + self.arrive[5].astype(F32)
        return jnp.concatenate([low, high], axis=-1)

    def drain(self):
        for copy in self.inner + self.outer:
            copy.wait_send()

    def run(self):
        self.start()
        self.relay()
        total = self.finish()
        self.drain()
        return total


GATHER_SEMS = [pltpu.SemaphoreType.DMA((13,)), pltpu.SemaphoreType.DMA((13,))]
SCATTER_SEMS = [pltpu.SemaphoreType.DMA((10,)), pltpu.SemaphoreType.DMA((10,))]


def scatter_scratch(rows, dim):
    return [pltpu.VMEM((CHIPS, rows, dim), BF), pltpu.VMEM((6, rows, dim // 2), BF),
            pltpu.VMEM((6, rows, dim // 2), BF)] + SCATTER_SEMS


def put_part(part, value, col):
    rows, width = part.shape[2], value.shape[1]
    for b in range(CHIPS * CORES):
        part[b % CORES, b // CORES, :, pl.ds(col, width)] = value[b * rows:(b + 1) * rows].astype(BF)


def norm_stats(hidden_f):
    inv_rms = lax.rsqrt(jnp.mean(hidden_f * hidden_f, axis=-1, keepdims=True) + RMS_EPS)
    return hidden_f * inv_rms, inv_rms


def norm_bwd(grad_f, normed, inv_rms, gain):
    gain_part = jnp.sum(grad_f * normed, axis=0, keepdims=True)
    scaled = grad_f * gain
    return inv_rms * (scaled - normed * jnp.mean(scaled * normed, axis=-1, keepdims=True)), gain_part


def rope(values, cos2, sin2):
    return values * cos2 + pltpu.roll(values, values.shape[-1] // 2, axis=1) * sin2


def full(buf):
    blocks, rows, dim = buf.shape
    return buf[...].reshape(blocks * rows, dim)


def lookup_kernel(group_ids, pick_ref, emb_hbm, out_ref, groups, sem):
    count = groups.shape[0]

    @pl.loop(0, count)
    def _(i):
        pltpu.make_async_copy(emb_hbm.at[pl.ds(pl.multiple_of(group_ids[i] * 8, 8), 8)], groups.at[i], sem).start()

    pltpu.make_async_copy(groups, groups, sem).wait()
    seq = pick_ref.shape[0]
    col = lax.broadcasted_iota(jnp.int32, (seq, count * 8), 1)
    pick = jnp.where(col == pick_ref[...], 1.0, 0.0).astype(BF)
    dim = groups.shape[2]
    step = 512

    @pl.loop(0, dim // step)
    def _(j):
        cols = pl.ds(pl.multiple_of(j * step, step), step)
        block = groups[:, :, cols].reshape(count * 8, step)
        out_ref[:, cols] = dot(pick, block).astype(BF)


def lookup(tokens, emb):
    rows_local, dim = emb.shape
    seq = tokens.shape[0]
    order = jnp.transpose(tokens.reshape(CHIPS, CORES, -1), (1, 0, 2)).reshape(-1)
    local = order - lax.axis_index('tp') * rows_local
    owned = (local >= 0) & (local < rows_local)
    safe = jnp.clip(local, 0, rows_local - 1)
    pick = jnp.where(owned, jnp.arange(seq, dtype=jnp.int32) * 8 + safe % 8, -1)
    return pl.pallas_call(
        lookup_kernel,
        out_shape=jax.ShapeDtypeStruct((seq, dim), BF),
        grid_spec=pltpu.PrefetchScalarGridSpec(
            num_scalar_prefetch=1, grid=(),
            in_specs=[pl.BlockSpec(memory_space=pltpu.VMEM), pl.BlockSpec(memory_space=pltpu.HBM)],
            out_specs=pl.BlockSpec(memory_space=pltpu.VMEM),
            scratch_shapes=[pltpu.VMEM((seq, 8, dim), BF), pltpu.SemaphoreType.DMA]),
        compiler_params=pltpu.CompilerParams(vmem_limit_bytes=40 << 20),
        name='lookup',
    )((safe // 8).astype(jnp.int32), pick[:, None], emb)


def forward_kernel(emb_part, cos_ref, sin_ref, gain_attn, gain_mlp, grad_own,
                   wq_hbm, wk_hbm, wv_hbm, wo_hbm, wg_hbm, wu_hbm, wd_hbm,
                   x0_out, h1_out, n1_out, n2_out, gh_out, heads_out, q_out, k_out, v_out, probs_out,
                   act_out, dgate_out, dup_out, dn2_part,
                   wqkv, wo, wg, wu, wd, wsem, n1_buf, n2_buf, gh_buf, attn_part, gact,
                   rp1, wk1, ar1, ss1, rs1, rp2, wk2, ar2, ss2, rs2,
                   gs1, gr1, gs2, gr2, gs0, gr0):
    pos = Place()
    num_heads, dim, head_dim = wq_hbm.shape
    seq = n1_out.shape[0]
    ffn = wg.shape[1]
    loads = [pltpu.make_async_copy(wq_hbm.at[h], wqkv.at[:, pl.ds(h * head_dim, head_dim)], wsem.at[h])
             for h in range(num_heads)]
    loads.append(pltpu.make_async_copy(wk_hbm, wqkv.at[:, pl.ds(num_heads * head_dim, head_dim)], wsem.at[3]))
    loads.append(pltpu.make_async_copy(wv_hbm, wqkv.at[:, pl.ds((num_heads + 1) * head_dim, head_dim)], wsem.at[4]))
    for k, (src, dst) in enumerate(((wo_hbm, wo), (wd_hbm, wd), (wg_hbm, wg), (wu_hbm, wu))):
        loads.append(pltpu.make_async_copy(src, dst, wsem.at[5 + k]))
    for load in loads:
        load.start()
    entry_barrier(pos)

    first = Scatter(pos, emb_part, rp1, wk1, ar1, ss1, rs1).run()
    x0 = first
    x0_out[...] = x0.astype(BF)
    normed1, _ = norm_stats(x0)
    n1_buf[pos.me] = (normed1 * gain_attn[...]).astype(BF)
    gather1 = Gather(pos, n1_buf, gs1, gr1)
    gather1.run()

    gh_buf[pos.me] = grad_own[...]
    gather0 = Gather(pos, gh_buf, gs0, gr0)
    gather0.start()

    for load in loads[:5]:
        load.wait()
    n1 = full(n1_buf)
    qkv = dot(n1, wqkv[...])
    n1_out[...] = n1
    gather0.relay()
    cos2, sin2 = cos_ref[...], sin_ref[...]
    kq = num_heads * head_dim
    keys = rope(qkv[:, kq:kq + head_dim], cos2, sin2).astype(BF)
    values = qkv[:, kq + head_dim:].astype(BF)
    k_out[...] = keys
    v_out[...] = values
    row = lax.broadcasted_iota(jnp.int32, (seq, seq), 0)
    colm = lax.broadcasted_iota(jnp.int32, (seq, seq), 1)
    causal = row >= colm
    for h in range(num_heads):
        cols = slice(h * head_dim, (h + 1) * head_dim)
        query = rope(qkv[:, cols], cos2, sin2).astype(BF)
        q_out[:, cols] = query
        scores = jnp.where(causal, dot_bt(query, keys) * (head_dim ** -0.5), -1e30)
        top = jnp.max(scores, axis=-1, keepdims=True)
        expd = jnp.exp(scores - top)
        probs = expd / jnp.sum(expd, axis=-1, keepdims=True)
        probs_out[h] = probs
        heads_out[:, cols] = dot(probs.astype(BF), values).astype(BF)
    loads[5].wait()
    heads = heads_out[...]
    for j in range(dim // 512):
        put_part(attn_part, dot(heads, wo[:, j * 512:(j + 1) * 512]), j * 512)
    scatter2 = Scatter(pos, attn_part, rp2, wk2, ar2, ss2, rs2)
    scatter2.start()
    gather0.finish()
    scatter2.relay()

    loads[6].wait()
    gh = full(gh_buf)
    gh_out[...] = gh

    @pl.loop(0, ffn // 256)
    def _(j):
        rows = pl.ds(pl.multiple_of(j * 256, 256), 256)
        gact[:, rows] = dot_bt(gh_out[...], wd[rows, :]).astype(BF)

    attn_sum = scatter2.finish()
    h1 = (x0 + attn_sum).astype(BF)
    h1_out[...] = h1
    normed2, _ = norm_stats(h1.astype(F32))
    n2_buf[pos.me] = (normed2 * gain_mlp[...]).astype(BF)
    gather2 = Gather(pos, n2_buf, gs2, gr2)
    gather2.start()
    gather2.relay()
    loads[7].wait()
    loads[8].wait()
    gather2.finish()

    n2_out[...] = full(n2_buf)

    @pl.loop(0, ffn // 256)
    def _(j):
        cols = pl.ds(pl.multiple_of(j * 256, 256), 256)
        n2 = n2_out[...]
        gate_pre = dot(n2, wg[:, cols])
        up_pre = dot(n2, wu[:, cols])
        sig = jax.nn.sigmoid(gate_pre)
        gate_act = gate_pre * sig
        act_out[:, cols] = (gate_act * up_pre).astype(BF)
        grad_act = gact[:, cols].astype(F32)
        dup_out[:, cols] = (grad_act * gate_act).astype(BF)
        dgate_out[:, cols] = (grad_act * up_pre * sig * (1.0 + gate_pre * (1.0 - sig))).astype(BF)

    @pl.loop(0, dim // 512)
    def _(j):
        col = pl.multiple_of(j * 512, 512)
        rows = pl.ds(col, 512)
        put_part(dn2_part, dot_bt(dgate_out[...], wg[rows, :]) + dot_bt(dup_out[...], wu[rows, :]), col)

    gather0.drain()
    scatter2.drain()
    gather2.drain()


def forward(emb_part, cos2, sin2, gain_attn, gain_mlp, grad_own, wq, wk, wv, wo, wg, wu, wd):
    num_heads, dim, head_dim = wq.shape
    seq, ffn = cos2.shape[0], wg.shape[1]
    rows = seq // (CHIPS * CORES)
    vmem = pl.BlockSpec(memory_space=pltpu.VMEM)
    hbm = pl.BlockSpec(memory_space=pltpu.HBM)
    width = num_heads * head_dim
    sds = jax.ShapeDtypeStruct
    outs = [sds((rows, dim), BF), sds((rows, dim), BF), sds((seq, dim), BF), sds((seq, dim), BF), sds((seq, dim), BF),
            sds((seq, width), BF), sds((seq, width), BF), sds((seq, head_dim), BF), sds((seq, head_dim), BF),
            sds((num_heads, seq, seq), F32), sds((seq, ffn), BF), sds((seq, ffn), BF), sds((seq, ffn), BF),
            sds((CORES, CHIPS, rows, dim), BF)]
    scratch = [pltpu.VMEM((dim, width + 2 * head_dim), BF), pltpu.VMEM((width, dim), BF), pltpu.VMEM((dim, ffn), BF),
               pltpu.VMEM((dim, ffn), BF), pltpu.VMEM((ffn, dim), BF), pltpu.SemaphoreType.DMA((9,)),
               pltpu.VMEM((CHIPS * CORES, rows, dim), BF), pltpu.VMEM((CHIPS * CORES, rows, dim), BF),
               pltpu.VMEM((CHIPS * CORES, rows, dim), BF), pltpu.VMEM((CORES, CHIPS, rows, dim), BF),
               pltpu.VMEM((seq, ffn), BF)]
    scratch += scatter_scratch(rows, dim) + scatter_scratch(rows, dim) + GATHER_SEMS * 3
    return pl.pallas_call(
        forward_kernel, out_shape=outs, in_specs=[vmem] * 6 + [hbm] * 7, out_specs=[vmem] * len(outs),
        scratch_shapes=scratch,
        compiler_params=pltpu.CompilerParams(collective_id=0, has_side_effects=True, vmem_limit_bytes=56 << 20),
        name='forward',
    )(emb_part, cos2, sin2, gain_attn, gain_mlp, grad_own, wq, wk, wv, wo, wg, wu, wd)


def backward_kernel(dn2_part, act_ref, x0_ref, h1_ref, grad_own, cos_ref, sin_ref, gain_attn, gain_mlp,
                    q_ref, k_ref, v_ref, probs_ref, wq_hbm, wk_hbm, wv_hbm, wo_hbm, wd_hbm,
                    hidden_out, dh1_out, dqkv_out, dx_out, gains_out,
                    wqkv, wo, wd, wsem, dh1_buf, dx_buf, gain_buf, mlp_part, dn1_part,
                    rp6, wk6, ar6, ss6, rs6, rp5, wk5, ar5, ss5, rs5, rp8, wk8, ar8, ss8, rs8,
                    gs7, gr7, gs9, gr9, gsg, grg):
    pos = Place()
    num_heads, dim, head_dim = wq_hbm.shape
    seq, ffn = act_ref.shape
    loads = [pltpu.make_async_copy(wd_hbm, wd, wsem.at[0]), pltpu.make_async_copy(wo_hbm, wo, wsem.at[1])]
    loads += [pltpu.make_async_copy(wq_hbm.at[h], wqkv.at[:, pl.ds(h * head_dim, head_dim)], wsem.at[2 + h])
              for h in range(num_heads)]
    loads.append(pltpu.make_async_copy(wk_hbm, wqkv.at[:, pl.ds(num_heads * head_dim, head_dim)], wsem.at[5]))
    loads.append(pltpu.make_async_copy(wv_hbm, wqkv.at[:, pl.ds((num_heads + 1) * head_dim, head_dim)], wsem.at[6]))
    for load in loads:
        load.start()
    entry_barrier(pos)

    scatter6 = Scatter(pos, dn2_part, rp6, wk6, ar6, ss6, rs6)
    scatter6.start()
    scatter6.relay()
    h1 = h1_ref[...].astype(F32)
    normed2, inv2 = norm_stats(h1)
    grad_n2 = scatter6.finish().astype(BF).astype(F32)
    grad_h1_norm, gain_mlp_part = norm_bwd(grad_n2, normed2, inv2, gain_mlp[...])
    grad_h1 = (grad_own[...].astype(F32) + grad_h1_norm).astype(BF)
    dh1_buf[pos.me] = grad_h1
    gain_buf[pos.me, 1:2, :] = gain_mlp_part
    gather7 = Gather(pos, dh1_buf, gs7, gr7)
    gather7.start()
    gather7.relay()

    loads[0].wait()

    @pl.loop(0, dim // 512)
    def _(j):
        col = pl.multiple_of(j * 512, 512)
        put_part(mlp_part, dot(act_ref[...], wd[:, pl.ds(col, 512)]), col)

    gather7.finish()
    scatter5 = Scatter(pos, mlp_part, rp5, wk5, ar5, ss5, rs5)
    scatter5.start()

    loads[1].wait()
    dh1 = full(dh1_buf)
    dh1_out[...] = dh1
    dheads = dot_bt(dh1, wo[...]).astype(BF)
    scatter5.relay()
    keys, values = k_ref[...], v_ref[...]
    cos2, nsin2 = cos_ref[...], -sin_ref[...]
    dkeys = jnp.zeros((seq, head_dim), F32)
    dvalues = jnp.zeros((seq, head_dim), F32)
    for h in range(num_heads):
        cols = slice(h * head_dim, (h + 1) * head_dim)
        dhead = dheads[:, cols]
        probs = probs_ref[h]
        dprobs = dot_bt(dhead, values).astype(BF).astype(F32)
        dvalues += dot_at(probs.astype(BF), dhead)
        inner = jnp.sum(dprobs * probs, axis=-1, keepdims=True)
        dscores = (probs * (dprobs - inner) * (head_dim ** -0.5)).astype(BF)
        dquery = dot(dscores, keys).astype(BF)
        dkeys += dot_at(dscores, q_ref[:, cols])
        dqkv_out[:, cols] = rope(dquery.astype(F32), cos2, nsin2).astype(BF)
    kq = num_heads * head_dim
    dqkv_out[:, kq:kq + head_dim] = rope(dkeys.astype(BF).astype(F32), cos2, nsin2).astype(BF)
    dqkv_out[:, kq + head_dim:] = dvalues.astype(BF)
    for load in loads[2:]:
        load.wait()

    @pl.loop(0, dim // 512)
    def _(j):
        col = pl.multiple_of(j * 512, 512)
        put_part(dn1_part, dot_bt(dqkv_out[...], wqkv[pl.ds(col, 512), :]), col)

    scatter8 = Scatter(pos, dn1_part, rp8, wk8, ar8, ss8, rs8)
    scatter8.start()
    hidden_out[...] = (h1 + scatter5.finish()).astype(BF)
    scatter8.relay()
    normed1, inv1 = norm_stats(x0_ref[...].astype(F32))
    grad_n1 = scatter8.finish().astype(BF).astype(F32)
    grad_x_norm, gain_attn_part = norm_bwd(grad_n1, normed1, inv1, gain_attn[...])
    dx_buf[pos.me] = (dh1_buf[pos.me].astype(F32) + grad_x_norm).astype(BF)
    gain_buf[pos.me, 0:1, :] = gain_attn_part
    gather9 = Gather(pos, dx_buf, gs9, gr9)
    gatherg = Gather(pos, gain_buf, gsg, grg)
    gather9.start()
    gatherg.start()
    gather9.relay()
    gatherg.relay()
    gather9.finish()
    gatherg.finish()
    dx_out[...] = full(dx_buf)
    total = gain_buf[0]
    for i in range(1, CHIPS * CORES):
        total = total + gain_buf[i]
    gains_out[...] = total
    for op in (scatter6, gather7, scatter5, scatter8, gather9, gatherg):
        op.drain()


def backward(dn2_part, act, x0, h1, grad_own, cos2, sin2, gain_attn, gain_mlp, q, k, v, probs, wq, wk, wv, wo, wd):
    num_heads, dim, head_dim = wq.shape
    seq, ffn = act.shape
    rows = seq // (CHIPS * CORES)
    blocks = CHIPS * CORES
    vmem = pl.BlockSpec(memory_space=pltpu.VMEM)
    hbm = pl.BlockSpec(memory_space=pltpu.HBM)
    width = num_heads * head_dim
    sds = jax.ShapeDtypeStruct
    outs = [sds((rows, dim), BF), sds((seq, dim), BF), sds((seq, width + 2 * head_dim), BF), sds((seq, dim), BF),
            sds((2, dim), F32)]
    scratch = [pltpu.VMEM((dim, width + 2 * head_dim), BF), pltpu.VMEM((width, dim), BF), pltpu.VMEM((ffn, dim), BF),
               pltpu.SemaphoreType.DMA((7,)),
               pltpu.VMEM((blocks, rows, dim), BF), pltpu.VMEM((blocks, rows, dim), BF),
               pltpu.VMEM((blocks, 2, dim), F32), pltpu.VMEM((CORES, CHIPS, rows, dim), BF),
               pltpu.VMEM((CORES, CHIPS, rows, dim), BF)]
    scratch += scatter_scratch(rows, dim) * 3 + GATHER_SEMS * 3
    return pl.pallas_call(
        backward_kernel, out_shape=outs, in_specs=[vmem] * 13 + [hbm] * 5, out_specs=[vmem] * len(outs),
        scratch_shapes=scratch,
        compiler_params=pltpu.CompilerParams(collective_id=1, has_side_effects=True, vmem_limit_bytes=40 << 20),
        name='backward',
    )(dn2_part, act, x0, h1, grad_own, cos2, sin2, gain_attn, gain_mlp, q, k, v, probs, wq, wk, wv, wo, wd)


def mlp_grads_kernel(n2, dgate, dup, act, gh, gw_gate, gw_up, gw_down):
    gw_gate[...] = dot_at(n2[...], dgate[...])
    gw_up[...] = dot_at(n2[...], dup[...])
    gw_down[...] = dot_at(act[...], gh[...])


def mlp_grads(n2, dgate, dup, act, gh):
    seq, dim = n2.shape
    ffn = act.shape[1]
    steps = 8
    sds = jax.ShapeDtypeStruct
    return pl.pallas_call(
        mlp_grads_kernel, grid=(steps,),
        out_shape=[sds((dim, ffn), F32), sds((dim, ffn), F32), sds((ffn, dim), F32)],
        in_specs=[pl.BlockSpec((seq, dim // steps), lambda i: (0, i)), pl.BlockSpec((seq, ffn), lambda i: (0, 0)),
                  pl.BlockSpec((seq, ffn), lambda i: (0, 0)), pl.BlockSpec((seq, ffn // steps), lambda i: (0, i)),
                  pl.BlockSpec((seq, dim), lambda i: (0, 0))],
        out_specs=[pl.BlockSpec((dim // steps, ffn), lambda i: (i, 0)), pl.BlockSpec((dim // steps, ffn), lambda i: (i, 0)),
                   pl.BlockSpec((ffn // steps, dim), lambda i: (i, 0))],
        compiler_params=pltpu.CompilerParams(vmem_limit_bytes=40 << 20),
        name='mlp_grads',
    )(n2, dgate, dup, act, gh)


def rest_grads_kernel(n1, dqkv, heads, dh1, ids, dx, gw_query, gw_key, gw_value, gw_out, g_emb):
    num_heads, _, head_dim = gw_query.shape
    width = num_heads * head_dim
    both = dot_at(n1[...], dqkv[...])
    for h in range(num_heads):
        gw_query[h] = both[:, h * head_dim:(h + 1) * head_dim]
    gw_key[...] = both[:, width:width + head_dim]
    gw_value[...] = both[:, width + head_dim:]
    gw_out[...] = dot_at(heads[...], dh1[...])
    rows, seq = g_emb.shape[0], dx.shape[0]
    row = lax.broadcasted_iota(jnp.int32, (rows, seq), 0) + pl.program_id(0) * rows
    pick = jnp.where(row == ids[...], 1.0, 0.0).astype(BF)
    g_emb[...] = dot(pick, dx[...])


def rest_grads(n1, dqkv, heads, dh1, ids, dx, rows_local, head_dim):
    seq, dim = n1.shape
    width = heads.shape[1]
    num_heads = width // head_dim
    sds = jax.ShapeDtypeStruct
    return pl.pallas_call(
        rest_grads_kernel, grid=(8,),
        out_shape=[sds((num_heads, dim, head_dim), F32), sds((dim, head_dim), F32), sds((dim, head_dim), F32),
                   sds((width, dim), F32), sds((rows_local, dim), F32)],
        in_specs=[pl.BlockSpec((seq, dim // 8), lambda i: (0, i)), pl.BlockSpec((seq, dqkv.shape[1]), lambda i: (0, 0)),
                  pl.BlockSpec((seq, width), lambda i: (0, 0)), pl.BlockSpec((seq, dim // 8), lambda i: (0, i)),
                  pl.BlockSpec((1, seq), lambda i: (0, 0)), pl.BlockSpec((seq, dim), lambda i: (0, 0))],
        out_specs=[pl.BlockSpec((num_heads, dim // 8, head_dim), lambda i: (0, i, 0)),
                   pl.BlockSpec((dim // 8, head_dim), lambda i: (i, 0)), pl.BlockSpec((dim // 8, head_dim), lambda i: (i, 0)),
                   pl.BlockSpec((width, dim // 8), lambda i: (0, i)), pl.BlockSpec((rows_local // 8, dim), lambda i: (i, 0))],
        compiler_params=pltpu.CompilerParams(vmem_limit_bytes=40 << 20),
        name='rest_grads',
    )(n1, dqkv, heads, dh1, ids, dx)


def solution(mesh):
    if mesh.shape['tp'] != CHIPS * CORES:
        raise ValueError('tp size')
    in_specs = (P('dp', None), P('dp', None), P('tp', None), P(None), P(None),
                P(None, 'tp', None), P(None, 'tp', None), P(None, 'tp', None), P('tp', None, None),
                P(None, 'tp'), P(None, 'tp'), P('tp', None), P('dp', 'tp', None))
    out_specs = (P('dp', 'tp', None), P(('dp', 'tp'), None),
                 P('dp', 'tp', None), P('dp', 'tp', None), P('dp', 'tp', None), P(('dp', 'tp'), None, None),
                 P('dp', 'tp'), P('dp', 'tp'), P(('dp', 'tp'), None), P('dp'), P('dp'))

    def device_fn(tokens, positions, emb_shard, gain_attn, gain_mlp, w_query, w_key, w_value, w_out, w_gate, w_up, w_down, grad_hidden):
        rows_local, dim = emb_shard.shape
        seq = tokens.shape[1]
        rows = seq // (CHIPS * CORES)
        num_heads, head_dim = w_query.shape[1], w_query.shape[2]
        half_dim = head_dim // 2
        inv_freq = ROPE_THETA ** (-jnp.arange(half_dim, dtype=F32) * (2.0 / head_dim))
        angles = positions[0].astype(F32)[:, None] * inv_freq
        cos_tab, sin_tab = jnp.cos(angles), jnp.sin(angles)
        cos2 = jnp.concatenate([cos_tab, cos_tab], axis=1)
        sin2 = jnp.concatenate([-sin_tab, sin_tab], axis=1)
        wq = jnp.transpose(w_query, (1, 0, 2))
        wk, wv = w_key.reshape(dim, head_dim), w_value.reshape(dim, head_dim)
        wo = w_out.reshape(num_heads * head_dim, dim)
        ga, gm = gain_attn[None, :], gain_mlp[None, :]
        grad_own = grad_hidden[0]

        emb_part = lookup(tokens[0], emb_shard).reshape(CORES, CHIPS, rows, dim)
        (x0, h1, n1, n2, gh, heads, q, k, v, probs, act, dgate, dup, dn2_part) = forward(
            emb_part, cos2, sin2, ga, gm, grad_own, wq, wk, wv, wo, w_gate, w_up, w_down)
        gw_gate, gw_up, gw_down = mlp_grads(n2, dgate, dup, act, gh)
        hidden, dh1, dqkv, dx, gains = backward(
            dn2_part, act, x0, h1, grad_own, cos2, sin2, ga, gm, q, k, v, probs, wq, wk, wv, wo, w_down)
        local_ids = tokens - lax.axis_index('tp') * rows_local
        gw_query, gw_key, gw_value, gw_out, g_emb = rest_grads(n1, dqkv, heads, dh1, local_ids, dx, rows_local, head_dim)
        return (hidden[None], g_emb, jnp.transpose(gw_query, (1, 0, 2)), gw_key.reshape(dim, 1, head_dim),
                gw_value.reshape(dim, 1, head_dim), gw_out.reshape(num_heads, head_dim, dim),
                gw_gate, gw_up, gw_down, gains[0], gains[1])

    return jax.shard_map(device_fn, mesh=mesh, in_specs=in_specs, out_specs=out_specs, check_vma=False)
```

profile of v0, /device:TPU:113, one launch (start us, length us, event | category | flops | bytes accessed | tf_op | source)
XLA Modules:
  0.0 157.6 jit_solution(4200820855584244604)
XLA Ops:
  0.6 0.7 and_reduce_fusion
  1.3 0.1 min.18
  1.4 0.1 min.20
  1.5 0.1 reshape.160
  1.6 0.1 and.46
  1.7 0.1 min.22
  1.9 0.0 copy-start
  1.9 4.6 %copy-done = bf16[2048,3072]{1,0:T(8,128)(2,1)S(1)} copy-done((bf16[2048,3072]{1,0:T(8,128)(2,1)S(1)}, bf16[2048,3072]{1,0:T(8,128)(2,1)}, u32[]{:S(2)}) %copy-start) | copy-done | bytes 12582936
  6.5 11.9 %lookup.1 = bf16[128,3072]{1,0:T(8,128)(2,1)S(1)} custom-call(s32[128]{0:T(128)S(1)} %and_select_fusion.group_ids, s32[128,1]{1,0:T(8,128)S(1)} %fusion.2.pick_ref, bf16[2048,3072]{1,0:T(8,128)(2,1)S(1)} %copy-done), custom_call_target="tpu_custom_call" | custom-call | tf_op jit(solution)/shard_map/lookup/pallas_call | solution.py:235
  18.4 0.0 copy-start.5
  18.4 0.9 copy-done.5
  19.3 0.0 copy-done.25
  19.3 0.3 fusion.3
  19.6 0.8 pad_maximum_fusion
  20.4 0.0 copy-start.1
  20.4 0.0 copy-start.2
  20.4 0.0 copy-start.3
  20.4 0.0 copy-start.4
  20.4 0.0 copy-start.11
  20.4 0.0 copy-start.12
  20.4 0.0 copy-start.13
  20.5 0.0 copy-start.21
  20.5 0.0 copy-start.22
  20.5 55.9 %forward.1 = (bf16[16,3072]{1,0:T(8,128)(2,1)}, bf16[16,3072]{1,0:T(8,128)(2,1)}, bf16[128,3072]{1,0:T(8,128)(2,1)}, bf16[128,3072]{1,0:T(8,128)(2,1)}, bf16[128...) custom-call(bf16[2,4,16,3072]{3,2,1,0:T(8,128)(2,1)} %bitcast.31, ...), custom_call_target="tpu_custom_call" | custom-call | tf_op jit(solution)/shard_map/forward/pallas_call | solution.py:380
  76.4 0.0 copy-done.1
  76.4 0.0 copy-done.2
  76.5 0.0 copy-done.3
  76.5 0.0 copy-done.4
  76.5 0.0 copy-done.11
  76.5 0.0 copy-done.12
  76.5 0.0 copy-done.13
  76.5 0.0 copy-done.21
  76.5 0.0 copy-done.22
  76.5 0.0 copy-start.6
  76.5 0.9 copy-done.6
  77.5 0.0 copy-start.10
  77.5 1.1 copy-done.10
  78.6 0.0 copy-start.16
  78.6 0.9 copy-done.16
  79.5 0.0 copy-start.17
  79.5 0.9 copy-done.17
  80.4 0.0 copy-start.18
  80.4 0.9 copy-done.18
  81.3 0.9 copy-done.19
  82.2 0.0 copy-start.23
  82.2 0.8 copy-done.23
  83.0 0.0 copy-start.24
  83.0 0.8 copy-done.24
  83.7 0.0 copy-start.20
  83.7 0.0 copy-start.7
  83.7 0.0 copy-start.8
  83.7 0.0 copy-start.14
  83.8 0.0 copy-start.15
  83.8 46.3 %backward.1 = (bf16[16,3072]{1,0:T(8,128)(2,1)S(1)}, bf16[128,3072]{1,0:T(8,128)(2,1)S(1)}, bf16[128,640]{1,0:T(8,128)(2,1)S(1)}, bf16[128,3072]{1,0:T(8,128)(2,1)S(1)}, f32[2,3072]{1,0:T(2,128)S(1)}) custom-call(bf16[2,4,16,3072]{3,2,1,0:T(8,128)(2,1)S(1)} %copy-done.10, bf16[128,1024]{1,0:T(8,128)(2,1)S(1)} %copy-done.6, bf16[16,3072]{1,0:T(8,128)(2,1)S(1)} %copy-done.17, ...), custom_call_target="tpu_custom_call" | custom-call | tf_op jit(solution)/shard_map/backward/pallas_call | solution.py:505
  130.1 0.0 copy-done.9
  130.1 0.0 copy-done.20
  130.1 13.4 %rest_grads.1 = (f32[3,3072,128]{2,1,0:T(8,128)}, f32[3072,128]{1,0:T(8,128)}, f32[3072,128]{1,0:T(8,128)}, f32[384,3072]{1,0:T(8,128)}, f32[2048,3072]{1,0:T(8,128)}) custom-call(bf16[128,3072]{1,0:T(8,128)(2,1)S(1)} %copy-done.9, bf16[128,640]{1,0:T(8,128)(2,1)S(1)} %get-tuple-element.48.dqkv, bf16[128,384]{1,0:T(8,128)(2,1)S(1)} %copy-done.20, ...), custom_call_target="tpu_custom_call" | custom-call | tf_op jit(solution)/shard_map/rest_grads/pallas_call | solution.py:557
  143.5 0.0 copy-done.7
  143.5 0.0 copy-done.8
  143.5 0.0 copy-done.14
  143.5 0.0 copy-done.15
  143.5 12.8 %mlp_grads.1 = (f32[3072,1024]{1,0:T(8,128)}, f32[3072,1024]{1,0:T(8,128)}, f32[1024,3072]{1,0:T(8,128)}) custom-call(bf16[128,3072]{1,0:T(8,128)(2,1)S(1)} %copy-done.7, bf16[128,1024]{1,0:T(8,128)(2,1)S(1)} %copy-done.14, bf16[128,1024]{1,0:T(8,128)(2,1)S(1)} %copy-done.15, bf16[128,1024]{1,0:T(8,128)(2,1)S(1)} %copy-done.6, bf16[128,3072]{1,0:T(8,128)(2,1)S(1)} %copy-done.8), custom_call_target="tpu_custom_call" | custom-call | tf_op jit(solution)/shard_map/mlp_grads/pallas_call | solution.py:524
  156.3 0.6 fusion.4
  157.0 0.6 copy.43
  (10 shorter events, 0.1 us)
Async XLA Ops:
  1.9 4.6 %copy-start = (bf16[2048,3072]{1,0:T(8,128)(2,1)S(1)}, bf16[2048,3072]{1,0:T(8,128)(2,1)}, u32[]{:S(2)}) copy-start(bf16[2048,3072]{1,0:T(8,128)(2,1)} %emb_hbm.1) | copy-start | bytes 37748740
  6.5 12.8 %copy-start.25 = (s32[1,128]{1,0:T(1,128)S(1)}, s32[1,128]{1,0:T(1,128)}, u32[]{:S(2)}) copy-start(s32[1,128]{1,0:T(1,128)} %param.14) | copy-start | bytes 1540
  18.4 0.9 copy-start.5
  20.4 56.0 %copy-start.1 = (bf16[3072,3,128]{2,0,1:T(8,128)(2,1)S(1)}, bf16[3072,3,128]{2,0,1:T(8,128)(2,1)}, u32[]{:S(2)}) copy-start(bf16[3072,3,128]{2,0,1:T(8,128)(2,1)} %param.18) | copy-start | bytes 7077892
  20.4 56.0 %copy-start.2 = (bf16[3,128,3072]{2,1,0:T(8,128)(2,1)S(1)}, bf16[3,128,3072]{2,1,0:T(8,128)(2,1)}, u32[]{:S(2)}) copy-start(bf16[3,128,3072]{2,1,0:T(8,128)(2,1)} %param.21) | copy-start | bytes 7077892
  20.4 56.0 %copy-start.3 = (bf16[3072,1,128]{2,0,1:T(8,128)(2,1)S(1)}, bf16[3072,1,128]{2,0,1:T(8,128)(2,1)}, u32[]{:S(2)}) copy-start(bf16[3072,1,128]{2,0,1:T(8,128)(2,1)} %param.19) | copy-start | bytes 2359300
  20.4 56.1 %copy-start.4 = (bf16[3072,1,128]{2,0,1:T(8,128)(2,1)S(1)}, bf16[3072,1,128]{2,0,1:T(8,128)(2,1)}, u32[]{:S(2)}) copy-start(bf16[3072,1,128]{2,0,1:T(8,128)(2,1)} %param.20) | copy-start | bytes 2359300
  20.4 56.1 %copy-start.11 = (f32[128,128]{1,0:T(8,128)S(1)}, f32[128,128]{1,0:T(8,128)}, u32[]{:S(2)}) copy-start(f32[128,128]{1,0:T(8,128)} %get-tuple-element.94.cos_ref) | copy-start | bytes 196612
  20.4 56.1 %copy-start.12 = (f32[128,128]{1,0:T(8,128)S(1)}, f32[128,128]{1,0:T(8,128)}, u32[]{:S(2)}) copy-start(f32[128,128]{1,0:T(8,128)} %get-tuple-element.95.sin_ref) | copy-start | bytes 196612
  20.4 56.1 %copy-start.13 = (bf16[1,16,3072]{2,1,0:T(8,128)(2,1)S(1)}, bf16[1,16,3072]{2,1,0:T(8,128)(2,1)}, u32[]{:S(2)}) copy-start(bf16[1,16,3072]{2,1,0:T(8,128)(2,1)} %param.25) | copy-start | bytes 294916
  20.5 56.1 %copy-start.21 = (f32[3072]{0:T(1024)S(1)}, f32[3072]{0:T(1024)}, u32[]{:S(2)}) copy-start(f32[3072]{0:T(1024)} %param.16) | copy-start | bytes 36868
  20.5 56.1 %copy-start.22 = (f32[3072]{0:T(1024)S(1)}, f32[3072]{0:T(1024)}, u32[]{:S(2)}) copy-start(f32[3072]{0:T(1024)} %param.17) | copy-start | bytes 36868
  76.5 1.0 copy-start.6
  77.5 1.1 copy-start.10
  78.6 0.9 copy-start.16
  79.5 0.9 copy-start.17
  80.4 0.9 copy-start.18
  81.3 0.9 copy-start.19
  82.2 0.8 copy-start.23
  83.0 0.8 copy-start.24
  83.7 46.3 %copy-start.9 = (bf16[128,3072]{1,0:T(8,128)(2,1)S(1)}, bf16[128,3072]{1,0:T(8,128)(2,1)}, u32[]{:S(2)}) copy-start(bf16[128,3072]{1,0:T(8,128)(2,1)} %get-tuple-element.47.n1) | copy-start | bytes 2359300
  83.7 46.3 %copy-start.20 = (bf16[128,384]{1,0:T(8,128)(2,1)S(1)}, bf16[128,384]{1,0:T(8,128)(2,1)}, u32[]{:S(2)}) copy-start(bf16[128,384]{1,0:T(8,128)(2,1)} %get-tuple-element.49.heads) | copy-start | bytes 294916
  83.7 59.8 %copy-start.7 = (bf16[128,3072]{1,0:T(8,128)(2,1)S(1)}, bf16[128,3072]{1,0:T(8,128)(2,1)}, u32[]{:S(2)}) copy-start(bf16[128,3072]{1,0:T(8,128)(2,1)} %get-tuple-element.57.n2) | copy-start | bytes 2359300
  83.7 59.8 %copy-start.8 = (bf16[128,3072]{1,0:T(8,128)(2,1)S(1)}, bf16[128,3072]{1,0:T(8,128)(2,1)}, u32[]{:S(2)}) copy-start(bf16[128,3072]{1,0:T(8,128)(2,1)} %get-tuple-element.60.gh) | copy-start | bytes 2359300
  83.7 59.8 %copy-start.14 = (bf16[128,1024]{1,0:T(8,128)(2,1)S(1)}, bf16[128,1024]{1,0:T(8,128)(2,1)}, u32[]{:S(2)}) copy-start(bf16[128,1024]{1,0:T(8,128)(2,1)} %get-tuple-element.58.dgate) | copy-start | bytes 786436
  83.8 59.8 %copy-start.15 = (bf16[128,1024]{1,0:T(8,128)(2,1)S(1)}, bf16[128,1024]{1,0:T(8,128)(2,1)}, u32[]{:S(2)}) copy-start(bf16[128,1024]{1,0:T(8,128)(2,1)} %get-tuple-element.59.dup) | copy-start | bytes 786436
where the time goes:
time: 158 us
  Pallas kernels  140 us (89%)
  local copies, waits for them, and re-layouts  14.4 us (9%)
  other arithmetic  1.83 us (1%)
    pallas_call x1, Pallas kernels, forward(): pl.pallas_call(forward_kernel, out_shape=outs, in_specs=[vmem] * 6 + [hbm...  55.9 us
    pallas_call x1, Pallas kernels, backward(): pl.pallas_call(backward_kernel, out_shape=outs, in_specs=[vmem] * 13 + [h...  46.3 us
    pallas_call x1, Pallas kernels, rest_grads(): pl.pallas_call(rest_grads_kernel, grid=(8,), out_shape=[sds((num_heads, d...  13.4 us
    unnamed x53, local copies, waits for them, and re-layouts  13.4 us
    pallas_call x1, Pallas kernels, mlp_grads(): pl.pallas_call(mlp_grads_kernel, grid=(steps,), out_shape=[sds((dim, ffn)...  12.8 us
    pallas_call x1, Pallas kernels, lookup(): pl.pallas_call(lookup_kernel, out_shape=jax.ShapeDtypeStruct((seq, dim),...  11.9 us

commit v1 on v0

v1 whole, which is shorter than its diff:
```python
import jax
import jax.numpy as jnp
import numpy as np
from jax import lax
from jax.experimental import pallas as pl
from jax.experimental.pallas import tpu as pltpu
from jax.sharding import PartitionSpec as P

ROPE_THETA = 1000000.0
RMS_EPS = 1e-5
BF = jnp.bfloat16
F32 = jnp.float32
VMEM_FULL = 67043328
CHIPS = 4
CORES = 2


def dot(a, b):
    return lax.dot_general(a, b, (((1,), (0,)), ((), ())), preferred_element_type=F32)


def dot_bt(a, b):
    return lax.dot_general(a, b, (((1,), (1,)), ((), ())), preferred_element_type=F32)


def dot_at(a, b):
    return lax.dot_general(a, b, (((0,), (0,)), ((), ())), preferred_element_type=F32)


class Place:
    def __init__(self):
        me = lax.axis_index('tp')
        self.chip, self.core = me // CORES, me % CORES
        self.right_chip = (self.chip + 1) % CHIPS
        self.left_chip = (self.chip + CHIPS - 1) % CHIPS
        self.far_chip = (self.chip + 2) % CHIPS
        self.me = me
        self.other = 1 - self.core
        self.partner = self.chip * CORES + self.other
        self.right = self.right_chip * CORES + self.core
        self.left = self.left_chip * CORES + self.core
        self.far = self.far_chip * CORES + self.core


def remote(src, dst, send, recv, device):
    return pltpu.make_async_remote_copy(src_ref=src, dst_ref=dst, send_sem=send, recv_sem=recv,
                                        device_id={'tp': device}, device_id_type=pl.DeviceIdType.MESH)


def entry_barrier(pos):
    barrier = pltpu.get_barrier_semaphore()
    for device in (pos.left, pos.right, pos.partner):
        pl.semaphore_signal(barrier, inc=1, device_id={'tp': device}, device_id_type=pl.DeviceIdType.MESH)
    pl.semaphore_wait(barrier, 3)


class Gather:
    def __init__(self, pos, buf, send, recv):
        self.pos, self.buf = pos, buf
        half = buf.shape[-1] // 2
        p = pos
        other = p.other - p.core

        def piece(slot, part):
            if part == 2:
                return buf.at[slot]
            return buf.at[slot, :, pl.ds(part * half, half)]

        def copy(index, slot, part, device):
            ref = piece(slot, part)
            return remote(ref, ref, send.at[index], recv.at[index], device)

        plan = {
            0: ((p.me, 0, p.right), (p.left, 0)), 1: ((p.me, 1, p.left), (p.right, 1)),
            2: ((p.me, 2, p.partner), (p.partner, 2)),
            3: ((p.me, 1, p.right), (p.left, 1)), 4: ((p.me, 0, p.left), (p.right, 0)),
            5: ((p.left, 0, p.right), (p.far, 0)), 6: ((p.right, 1, p.left), (p.far, 1)),
            7: ((p.left, 0, p.partner), (p.left + other, 0)), 8: ((p.right, 1, p.partner), (p.right + other, 1)),
            9: ((p.left, 1, p.partner), (p.left + other, 1)), 10: ((p.right, 0, p.partner), (p.right + other, 0)),
            11: ((p.far, 0, p.partner), (p.far + other, 0)), 12: ((p.far, 1, p.partner), (p.far + other, 1)),
        }
        self.out = {i: copy(i, *s) for i, (s, _) in plan.items()}
        self.into = {i: copy(i, slot, part, p.partner) for i, (_, (slot, part)) in plan.items()}

    def start(self):
        for i in (0, 1, 2, 3, 4):
            self.out[i].start()

    def relay(self):
        for i, onward in ((0, (5, 7)), (1, (6, 8)), (3, (9,)), (4, (10,))):
            self.into[i].wait_recv()
            for j in onward:
                self.out[j].start()

    def finish(self):
        for i, j in ((5, 11), (6, 12)):
            self.into[i].wait_recv()
            self.out[j].start()
        for i in (2, 7, 8, 9, 10, 11, 12):
            self.into[i].wait_recv()

    def drain(self):
        for i in range(13):
            self.out[i].wait_send()

    def run(self):
        self.start()
        self.relay()
        self.finish()
        self.drain()


class Scatter:
    def __init__(self, pos, part, from_partner, work, arrive, send, recv):
        p = pos
        self.pos, self.part, self.from_partner, self.work, self.arrive = p, part, from_partner, work, arrive
        self.half = work.shape[-1]
        self.chips = (p.far_chip, p.right_chip, p.left_chip, p.chip)
        self.inner = [remote(part.at[p.other, y], from_partner.at[y], send.at[k], recv.at[k], p.partner)
                      for k, y in enumerate(self.chips)]
        self.outer = [remote(work.at[k], arrive.at[k], send.at[4 + k], recv.at[4 + k], p.right if k % 2 == 0 else p.left)
                      for k in range(6)]

    def pair(self, k, part):
        cols = pl.ds(part * self.half, self.half)
        y = self.chips[k]
        return self.part[self.pos.core, y, :, cols].astype(F32) + self.from_partner[y, :, cols].astype(F32)

    def send_sum(self, k, value):
        self.work[k] = value.astype(BF)
        self.outer[k].start()

    def start(self):
        for copy in self.inner:
            copy.start()

    def relay(self):
        self.inner[0].wait_recv()
        self.send_sum(0, self.pair(0, 0))
        self.send_sum(1, self.pair(0, 1))
        self.inner[1].wait_recv()
        self.send_sum(2, self.pair(1, 1))
        self.inner[2].wait_recv()
        self.send_sum(3, self.pair(2, 0))
        self.outer[0].wait_recv()
        self.send_sum(4, self.pair(1, 0) + self.arrive[0].astype(F32))
        self.outer[1].wait_recv()
        self.send_sum(5, self.pair(2, 1) + self.arrive[1].astype(F32))

    def finish(self):
        self.inner[3].wait_recv()
        for k in (2, 3, 4, 5):
            self.outer[k].wait_recv()
        low = self.pair(3, 0) + self.arrive[3].astype(F32) + self.arrive[4].astype(F32)
        high = self.pair(3, 1) + self.arrive[2].astype(F32) + self.arrive[5].astype(F32)
        return jnp.concatenate([low, high], axis=-1)

    def drain(self):
        for copy in self.inner + self.outer:
            copy.wait_send()

    def run(self):
        self.start()
        self.relay()
        total = self.finish()
        self.drain()
        return total


GATHER_SEMS = [pltpu.SemaphoreType.DMA((13,)), pltpu.SemaphoreType.DMA((13,))]
SCATTER_SEMS = [pltpu.SemaphoreType.DMA((10,)), pltpu.SemaphoreType.DMA((10,))]


def scatter_scratch(rows, dim):
    return [pltpu.VMEM((CHIPS, rows, dim), BF), pltpu.VMEM((6, rows, dim // 2), BF),
            pltpu.VMEM((6, rows, dim // 2), BF)] + SCATTER_SEMS


def put_part(part, value, col):
    rows, width = part.shape[2], value.shape[1]
    for b in range(CHIPS * CORES):
        part[b % CORES, b // CORES, :, pl.ds(col, width)] = value[b * rows:(b + 1) * rows].astype(BF)


def norm_stats(hidden_f):
    inv_rms = lax.rsqrt(jnp.mean(hidden_f * hidden_f, axis=-1, keepdims=True) + RMS_EPS)
    return hidden_f * inv_rms, inv_rms


def norm_bwd(grad_f, normed, inv_rms, gain):
    gain_part = jnp.sum(grad_f * normed, axis=0, keepdims=True)
    scaled = grad_f * gain
    return inv_rms * (scaled - normed * jnp.mean(scaled * normed, axis=-1, keepdims=True)), gain_part


def rope(values, cos2, sin2):
    return values * cos2 + pltpu.roll(values, values.shape[-1] // 2, axis=1) * sin2


def full(buf):
    blocks, rows, dim = buf.shape
    return buf[...].reshape(blocks * rows, dim)


def lookup_kernel(ids_smem, ids_ref, pos_ref, freq_ref, emb_hbm, out_ref, cos_ref, sin_ref, groups, sem):
    count, _, dim = groups.shape
    rows_local = emb_hbm.shape[0]
    base = lax.axis_index('tp') * rows_local

    @pl.loop(0, count)
    def _(i):
        local = jnp.clip(ids_smem[0, i] - base, 0, rows_local - 1)
        start = pl.multiple_of((local // 8) * 8, 8)
        pltpu.make_async_copy(emb_hbm.at[pl.ds(start, 8)], groups.at[i], sem).start()

    head_dim = cos_ref.shape[1]
    angles = jnp.transpose(freq_ref[...] * pos_ref[...].astype(F32))
    cos_ref[...] = jnp.cos(angles)
    lane = lax.broadcasted_iota(jnp.int32, angles.shape, 1)
    sin = jnp.sin(angles)
    sin_ref[...] = jnp.where(lane < head_dim // 2, -sin, sin)

    local = ids_ref[...] - base
    owned = (local >= 0) & (local < rows_local)
    place = jnp.where(owned, lax.broadcasted_iota(jnp.int32, local.shape, 1) * 8 + local % 8, -1)
    pick = jnp.where(lax.broadcasted_iota(jnp.int32, (count * 8, count), 0) == place, 1.0, 0.0).astype(BF)
    step = 512
    pltpu.make_async_copy(groups, groups, sem).wait()

    @pl.loop(0, dim // step)
    def _(j):
        col = pl.multiple_of(j * step, step)
        block = groups[:, :, pl.ds(col, step)].reshape(count * 8, step)
        put_part(out_ref, dot_at(pick, block), col)


def lookup(tokens, positions, emb, head_dim):
    dim = emb.shape[1]
    seq = tokens.shape[1]
    half = head_dim // 2
    freq = np.float32(ROPE_THETA) ** (-np.arange(half, dtype=np.float32) * np.float32(2.0 / head_dim))
    freq = jnp.asarray(np.concatenate([freq, freq])[:, None], F32)
    vmem = pl.BlockSpec(memory_space=pltpu.VMEM)
    sds = jax.ShapeDtypeStruct
    return pl.pallas_call(
        lookup_kernel,
        out_shape=[sds((CORES, CHIPS, seq // (CHIPS * CORES), dim), BF), sds((seq, head_dim), F32), sds((seq, head_dim), F32)],
        grid_spec=pltpu.PrefetchScalarGridSpec(
            num_scalar_prefetch=1, grid=(),
            in_specs=[vmem, vmem, vmem, pl.BlockSpec(memory_space=pltpu.HBM)], out_specs=[vmem] * 3,
            scratch_shapes=[pltpu.VMEM((seq, 8, dim), BF), pltpu.SemaphoreType.DMA]),
        compiler_params=pltpu.CompilerParams(vmem_limit_bytes=VMEM_FULL),
        name='lookup',
    )(tokens, tokens, positions, freq, emb)


def layer_kernel(emb_hbm, cos_hbm, sin_hbm, gain_attn, gain_mlp, grad_own, wq_hbm, wk_hbm, wv_hbm, wo_hbm, wg_hbm, wu_hbm, wd_hbm,
                 hidden_out, gains_out, n1_out, n2_out, gh_out, dh1_out, dx_out, heads_out, act_out, dgate_out, dup_out, dqkv_out,
                 emb_part, cos_ref, sin_ref, wqkv, wo, wg, wu, wd, wsem, osem, n1_buf, n2_buf, gh_buf, dh1_buf, dx_buf, gain_buf,
                 attn_part, dn2_part, mlp_part, dn1_part, heads_buf, gact, act_buf, dgate_buf, dup_buf, dqkv_buf, q_buf, probs_buf,
                 *comm):
    pos = Place()
    num_heads, dim, head_dim = wq_hbm.shape
    blocks, rows, _ = n1_buf.shape
    seq, ffn = blocks * rows, wg.shape[1]
    scatters, gathers = comm[:25], comm[25:]
    kq = num_heads * head_dim
    pairs = [(emb_hbm, emb_part), (cos_hbm, cos_ref), (sin_hbm, sin_ref)]
    pairs += [(wq_hbm.at[h], wqkv.at[:, pl.ds(h * head_dim, head_dim)]) for h in range(num_heads)]
    pairs += [(wk_hbm, wqkv.at[:, pl.ds(kq, head_dim)]), (wv_hbm, wqkv.at[:, pl.ds(kq + head_dim, head_dim)])]
    pairs += [(wo_hbm, wo), (wd_hbm, wd), (wg_hbm, wg), (wu_hbm, wu)]
    loads = [pltpu.make_async_copy(src, dst, wsem.at[k]) for k, (src, dst) in enumerate(pairs)]
    for load in loads:
        load.start()
    stores = []

    def store(src, dst):
        stores.append(pltpu.make_async_copy(src, dst, osem.at[len(stores)]))
        stores[-1].start()

    with jax.named_scope('barrier'):
        entry_barrier(pos)
        loads[0].wait()

    with jax.named_scope('rs1'):
        scatter1 = Scatter(pos, emb_part, *scatters[0:5])
        x0 = scatter1.run()
    with jax.named_scope('norm1'):
        normed1, inv1 = norm_stats(x0)
        n1_buf[pos.me] = (normed1 * gain_attn[...]).astype(BF)
    with jax.named_scope('ag1'):
        gather1 = Gather(pos, n1_buf, *gathers[0:2])
        gather1.run()
    store(n1_buf, n1_out)

    gh_buf[pos.me] = grad_own[...]
    gather0 = Gather(pos, gh_buf, *gathers[2:4])
    gather0.start()

    with jax.named_scope('wait_qkv'):
        for load in loads[1:8]:
            load.wait()
    with jax.named_scope('qkv'):
        qkv = dot(full(n1_buf), wqkv[...])
    with jax.named_scope('ag0_relay'):
        gather0.relay()
    with jax.named_scope('attention'):
        cos2, sin2 = cos_ref[...], sin_ref[...]
        keys = rope(qkv[:, kq:kq + head_dim], cos2, sin2).astype(BF)
        values = qkv[:, kq + head_dim:].astype(BF)
        causal = lax.broadcasted_iota(jnp.int32, (seq, seq), 0) >= lax.broadcasted_iota(jnp.int32, (seq, seq), 1)
        for h in range(num_heads):
            cols = slice(h * head_dim, (h + 1) * head_dim)
            query = rope(qkv[:, cols], cos2, sin2).astype(BF)
            q_buf[:, cols] = query
            scores = jnp.where(causal, dot_bt(query, keys) * (head_dim ** -0.5), -1e30)
            expd = jnp.exp(scores - jnp.max(scores, axis=-1, keepdims=True))
            probs = expd / jnp.sum(expd, axis=-1, keepdims=True)
            probs_buf[h] = probs
            heads_buf[:, cols] = dot(probs.astype(BF), values).astype(BF)
    store(heads_buf, heads_out)
    with jax.named_scope('w_out'):
        loads[8].wait()

        @pl.loop(0, dim // 512)
        def _(j):
            cols = pl.ds(pl.multiple_of(j * 512, 512), 512)
            put_part(attn_part, dot(heads_buf[...], wo[:, cols]), cols.start)

    with jax.named_scope('rs3_a'):
        scatter3 = Scatter(pos, attn_part, *scatters[5:10])
        scatter3.start()
        gather0.finish()
        scatter3.relay()
    store(gh_buf, gh_out)

    with jax.named_scope('grad_act'):
        loads[9].wait()

        @pl.loop(0, ffn // 256)
        def _(j):
            cols = pl.ds(pl.multiple_of(j * 256, 256), 256)
            gact[:, cols] = dot_bt(full(gh_buf), wd[cols, :]).astype(BF)

    with jax.named_scope('rs3_b'):
        h1_bf = (x0 + scatter3.finish()).astype(BF)
    with jax.named_scope('norm2'):
        h1 = h1_bf.astype(F32)
        normed2, inv2 = norm_stats(h1)
        n2_buf[pos.me] = (normed2 * gain_mlp[...]).astype(BF)
    with jax.named_scope('ag4'):
        gather4 = Gather(pos, n2_buf, *gathers[4:6])
        gather4.run()
        loads[10].wait()
        loads[11].wait()
    store(n2_buf, n2_out)

    with jax.named_scope('gate_up'):
        @pl.loop(0, ffn // 256)
        def _(j):
            cols = pl.ds(pl.multiple_of(j * 256, 256), 256)
            n2 = full(n2_buf)
            gate_pre = dot(n2, wg[:, cols])
            up_pre = dot(n2, wu[:, cols])
            sig = jax.nn.sigmoid(gate_pre)
            gate_act = gate_pre * sig
            act_buf[:, cols] = (gate_act * up_pre).astype(BF)
            grad_act = gact[:, cols].astype(F32)
            dup_buf[:, cols] = (grad_act * gate_act).astype(BF)
            dgate_buf[:, cols] = (grad_act * up_pre * sig * (1.0 + gate_pre * (1.0 - sig))).astype(BF)

    store(act_buf, act_out)
    store(dgate_buf, dgate_out)
    store(dup_buf, dup_out)
    with jax.named_scope('dn2'):
        @pl.loop(0, dim // 512)
        def _(j):
            col = pl.multiple_of(j * 512, 512)
            put_part(dn2_part, dot_bt(dgate_buf[...], wg[pl.ds(col, 512), :]) + dot_bt(dup_buf[...], wu[pl.ds(col, 512), :]), col)

    with jax.named_scope('rs6_a'):
        scatter6 = Scatter(pos, dn2_part, *scatters[10:15])
        scatter6.start()
        scatter6.relay()
    with jax.named_scope('rs6_b'):
        grad_n2 = scatter6.finish().astype(BF).astype(F32)
    with jax.named_scope('norm2_bwd'):
        grad_h1_norm, gain_mlp_part = norm_bwd(grad_n2, normed2, inv2, gain_mlp[...])
        grad_h1 = (grad_own[...].astype(F32) + grad_h1_norm).astype(BF)
        dh1_buf[pos.me] = grad_h1
        gain_buf[pos.me, 1:2, :] = gain_mlp_part
    with jax.named_scope('ag7_a'):
        gather7 = Gather(pos, dh1_buf, *gathers[6:8])
        gather7.start()
        gather7.relay()

    with jax.named_scope('w_down'):
        @pl.loop(0, dim // 512)
        def _(j):
            col = pl.multiple_of(j * 512, 512)
            put_part(mlp_part, dot(act_buf[...], wd[:, pl.ds(col, 512)]), col)

    with jax.named_scope('ag7_b'):
        gather7.finish()
    store(dh1_buf, dh1_out)
    scatter5 = Scatter(pos, mlp_part, *scatters[15:20])
    scatter5.start()

    with jax.named_scope('dheads'):
        dheads = dot_bt(full(dh1_buf), wo[...]).astype(BF)
    with jax.named_scope('rs5_relay'):
        scatter5.relay()
    with jax.named_scope('attention_bwd'):
        nsin2 = -sin2
        dkeys = jnp.zeros((seq, head_dim), F32)
        dvalues = jnp.zeros((seq, head_dim), F32)
        for h in range(num_heads):
            cols = slice(h * head_dim, (h + 1) * head_dim)
            dhead = dheads[:, cols]
            probs = probs_buf[h]
            dprobs = dot_bt(dhead, values).astype(BF).astype(F32)
            dvalues += dot_at(probs.astype(BF), dhead)
            inner = jnp.sum(dprobs * probs, axis=-1, keepdims=True)
            dscores = (probs * (dprobs - inner) * (head_dim ** -0.5)).astype(BF)
            dquery = dot(dscores, keys).astype(BF)
            dkeys += dot_at(dscores, q_buf[:, cols])
            dqkv_buf[:, cols] = rope(dquery.astype(F32), cos2, nsin2).astype(BF)
        dqkv_buf[:, kq:kq + head_dim] = rope(dkeys.astype(BF).astype(F32), cos2, nsin2).astype(BF)
        dqkv_buf[:, kq + head_dim:] = dvalues.astype(BF)
    store(dqkv_buf, dqkv_out)

    with jax.named_scope('dn1'):
        @pl.loop(0, dim // 512)
        def _(j):
            col = pl.multiple_of(j * 512, 512)
            put_part(dn1_part, dot_bt(dqkv_buf[...], wqkv[pl.ds(col, 512), :]), col)

    with jax.named_scope('rs8'):
        scatter8 = Scatter(pos, dn1_part, *scatters[20:25])
        scatter8.start()
        hidden_out[...] = (h1 + scatter5.finish()).astype(BF)
        scatter8.relay()
        grad_n1 = scatter8.finish().astype(BF).astype(F32)
    with jax.named_scope('norm1_bwd'):
        grad_x_norm, gain_attn_part = norm_bwd(grad_n1, normed1, inv1, gain_attn[...])
        dx_buf[pos.me] = (grad_h1.astype(F32) + grad_x_norm).astype(BF)
        gain_buf[pos.me, 0:1, :] = gain_attn_part
    with jax.named_scope('ag9'):
        gather9 = Gather(pos, dx_buf, *gathers[8:10])
        gatherg = Gather(pos, gain_buf, *gathers[10:12])
        gather9.start()
        gatherg.start()
        gather9.relay()
        gatherg.relay()
        gather9.finish()
        store(dx_buf, dx_out)
        gatherg.finish()
    with jax.named_scope('tail'):
        total = gain_buf[0]
        for i in range(1, blocks):
            total = total + gain_buf[i]
        gains_out[...] = total
        for op in (gather0, scatter3, scatter6, gather7, scatter5, scatter8, gather9, gatherg):
            op.drain()
        for copy in stores:
            copy.wait()


def layer(emb_part, cos2, sin2, gain_attn, gain_mlp, grad_own, wq, wk, wv, wo, wg, wu, wd):
    num_heads, dim, head_dim = wq.shape
    blocks = CHIPS * CORES
    seq, ffn = cos2.shape[0], wg.shape[1]
    rows = seq // blocks
    vmem = pl.BlockSpec(memory_space=pltpu.VMEM)
    hbm = pl.BlockSpec(memory_space=pltpu.HBM)
    width = num_heads * head_dim
    wide = width + 2 * head_dim
    sds = jax.ShapeDtypeStruct
    outs = [sds((rows, dim), BF), sds((2, dim), F32)] + [sds((blocks, rows, dim), BF)] * 5
    outs += [sds((seq, width), BF)] + [sds((seq, ffn), BF)] * 3 + [sds((seq, wide), BF)]
    part = pltpu.VMEM((CORES, CHIPS, rows, dim), BF)
    gathered = pltpu.VMEM((blocks, rows, dim), BF)
    table = pltpu.VMEM((seq, head_dim), F32)
    scratch = [part, table, table, pltpu.VMEM((dim, wide), BF), pltpu.VMEM((width, dim), BF), pltpu.VMEM((dim, ffn), BF),
               pltpu.VMEM((dim, ffn), BF), pltpu.VMEM((ffn, dim), BF), pltpu.SemaphoreType.DMA((12,)), pltpu.SemaphoreType.DMA((10,))]
    scratch += [gathered] * 5 + [pltpu.VMEM((blocks, 2, dim), F32)] + [part] * 4 + [pltpu.VMEM((seq, width), BF)]
    scratch += [pltpu.VMEM((seq, ffn), BF)] * 4 + [pltpu.VMEM((seq, wide), BF), pltpu.VMEM((seq, width), BF),
                                                   pltpu.VMEM((num_heads, seq, seq), F32)]
    scratch += scatter_scratch(rows, dim) * 5 + GATHER_SEMS * 6
    return pl.pallas_call(
        layer_kernel, out_shape=outs, in_specs=[hbm] * 3 + [vmem] * 3 + [hbm] * 7, out_specs=[vmem] * 2 + [hbm] * 10,
        scratch_shapes=scratch,
        compiler_params=pltpu.CompilerParams(collective_id=0, has_side_effects=True, vmem_limit_bytes=VMEM_FULL),
        name='layer',
    )(emb_part, cos2, sin2, gain_attn, gain_mlp, grad_own, wq, wk, wv, wo, wg, wu, wd)


def mlp_grads_kernel(n2, dgate, dup, act, gh, gw_gate, gw_up, gw_down):
    gw_gate[...] = dot_at(n2[...], dgate[...])
    gw_up[...] = dot_at(n2[...], dup[...])
    gw_down[...] = dot_at(act[...], gh[...])


def mlp_grads(n2, dgate, dup, act, gh):
    seq, dim = n2.shape
    ffn = act.shape[1]
    steps = 8
    sds = jax.ShapeDtypeStruct
    return pl.pallas_call(
        mlp_grads_kernel, grid=(steps,),
        out_shape=[sds((dim, ffn), F32), sds((dim, ffn), F32), sds((ffn, dim), F32)],
        in_specs=[pl.BlockSpec((seq, dim // steps), lambda i: (0, i)), pl.BlockSpec((seq, ffn), lambda i: (0, 0)),
                  pl.BlockSpec((seq, ffn), lambda i: (0, 0)), pl.BlockSpec((seq, ffn // steps), lambda i: (0, i)),
                  pl.BlockSpec((seq, dim), lambda i: (0, 0))],
        out_specs=[pl.BlockSpec((dim // steps, ffn), lambda i: (i, 0)), pl.BlockSpec((dim // steps, ffn), lambda i: (i, 0)),
                   pl.BlockSpec((ffn // steps, dim), lambda i: (i, 0))],
        compiler_params=pltpu.CompilerParams(vmem_limit_bytes=VMEM_FULL),
        name='mlp_grads',
    )(n2, dgate, dup, act, gh)


def rest_grads_kernel(n1, dqkv, heads, dh1, tokens, dx, hidden_in, gains_in,
                      gw_query, gw_key, gw_value, gw_out, g_emb, hidden, g_attn, g_mlp):
    num_heads, _, head_dim = gw_query.shape
    width = num_heads * head_dim
    both = dot_at(n1[...], dqkv[...])
    for h in range(num_heads):
        gw_query[h] = both[:, h * head_dim:(h + 1) * head_dim]
    gw_key[...] = both[:, width:width + head_dim]
    gw_value[...] = both[:, width + head_dim:]
    gw_out[...] = dot_at(heads[...], dh1[...])
    rows, seq = g_emb.shape[0], dx.shape[0]
    steps = pl.num_programs(0)
    first = lax.axis_index('tp') * (rows * steps) + pl.program_id(0) * rows
    row = lax.broadcasted_iota(jnp.int32, (rows, seq), 0) + first
    pick = jnp.where(row == tokens[...], 1.0, 0.0).astype(BF)
    g_emb[...] = dot(pick, dx[...])

    @pl.when(pl.program_id(0) == 0)
    def _():
        hidden[...] = hidden_in[...]
        g_attn[...] = gains_in[0:1, :]
        g_mlp[...] = gains_in[1:2, :]


def rest_grads(n1, dqkv, heads, dh1, tokens, dx, hidden, gains, rows_local, head_dim):
    seq, dim = n1.shape
    width = heads.shape[1]
    num_heads = width // head_dim
    steps = 8
    sds = jax.ShapeDtypeStruct

    def whole(shape):
        return pl.BlockSpec(shape, lambda i: (0,) * len(shape))

    return pl.pallas_call(
        rest_grads_kernel, grid=(steps,),
        out_shape=[sds((num_heads, dim, head_dim), F32), sds((dim, head_dim), F32), sds((dim, head_dim), F32),
                   sds((width, dim), F32), sds((rows_local, dim), F32), sds(hidden.shape, BF), sds((1, dim), F32), sds((1, dim), F32)],
        in_specs=[pl.BlockSpec((seq, dim // steps), lambda i: (0, i)), whole(dqkv.shape), whole(heads.shape),
                  pl.BlockSpec((seq, dim // steps), lambda i: (0, i)), whole(tokens.shape), whole(dx.shape),
                  whole(hidden.shape), whole(gains.shape)],
        out_specs=[pl.BlockSpec((num_heads, dim // steps, head_dim), lambda i: (0, i, 0)),
                   pl.BlockSpec((dim // steps, head_dim), lambda i: (i, 0)), pl.BlockSpec((dim // steps, head_dim), lambda i: (i, 0)),
                   pl.BlockSpec((width, dim // steps), lambda i: (0, i)), pl.BlockSpec((rows_local // steps, dim), lambda i: (i, 0)),
                   whole(hidden.shape), whole((1, dim)), whole((1, dim))],
        compiler_params=pltpu.CompilerParams(vmem_limit_bytes=VMEM_FULL),
        name='rest_grads',
    )(n1, dqkv, heads, dh1, tokens, dx, hidden, gains)


def solution(mesh):
    if mesh.shape['tp'] != CHIPS * CORES:
        raise ValueError('tp size')
    in_specs = (P('dp', None), P('dp', None), P('tp', None), P(None), P(None),
                P(None, 'tp', None), P(None, 'tp', None), P(None, 'tp', None), P('tp', None, None),
                P(None, 'tp'), P(None, 'tp'), P('tp', None), P('dp', 'tp', None))
    out_specs = (P('dp', 'tp', None), P(('dp', 'tp'), None),
                 P('dp', 'tp', None), P('dp', 'tp', None), P('dp', 'tp', None), P(('dp', 'tp'), None, None),
                 P('dp', 'tp'), P('dp', 'tp'), P(('dp', 'tp'), None), P('dp'), P('dp'))

    def device_fn(tokens, positions, emb_shard, gain_attn, gain_mlp, w_query, w_key, w_value, w_out, w_gate, w_up, w_down, grad_hidden):
        rows_local, dim = emb_shard.shape
        seq = tokens.shape[1]
        num_heads, head_dim = w_query.shape[1], w_query.shape[2]
        wq = jnp.transpose(w_query, (1, 0, 2))
        wk, wv = w_key.reshape(dim, head_dim), w_value.reshape(dim, head_dim)
        wo = w_out.reshape(num_heads * head_dim, dim)

        emb_part, cos2, sin2 = lookup(tokens, positions, emb_shard, head_dim)
        hidden, gains, n1, n2, gh, dh1, dx, heads, act, dgate, dup, dqkv = layer(
            emb_part, cos2, sin2, gain_attn[None, :], gain_mlp[None, :], grad_hidden[0], wq, wk, wv, wo, w_gate, w_up, w_down)
        n1, n2, gh, dh1, dx = (x.reshape(seq, dim) for x in (n1, n2, gh, dh1, dx))
        gw_gate, gw_up, gw_down = mlp_grads(n2, dgate, dup, act, gh)
        gw_query, gw_key, gw_value, gw_out, g_emb, hidden, g_attn, g_mlp = rest_grads(
            n1, dqkv, heads, dh1, tokens, dx, hidden, gains, rows_local, head_dim)
        return (hidden[None], g_emb, jnp.transpose(gw_query, (1, 0, 2)), gw_key.reshape(dim, 1, head_dim),
                gw_value.reshape(dim, 1, head_dim), gw_out.reshape(num_heads, head_dim, dim),
                gw_gate, gw_up, gw_down, g_attn[0], g_mlp[0])

    return jax.shard_map(device_fn, mesh=mesh, in_specs=in_specs, out_specs=out_specs, check_vma=False)
```

time: 158 us -> 144 us (0.911)
  local copies, waits for them, and re-layouts: 14.4 us -> 0 us
  Pallas kernels: 140 us -> 143 us
  other arithmetic: 1.83 us -> 0 us
    unnamed x53 -> x0, local copies, waits for them, and re-layouts: 13.4 us -> none
    pallas_call x4 -> x3, Pallas kernels: 128 us -> 129 us  [the longest x1 104 us: layer(): pl.pallas_call(layer_kernel, out_shape=outs, in_specs=[hbm] * 3 + [vmem]...]
where the time goes in v1:
time: 144 us
  Pallas kernels  143 us (99%)
    pallas_call x1, Pallas kernels, layer(): pl.pallas_call(layer_kernel, out_shape=outs, in_specs=[hbm] * 3 + [vmem]...  104 us
    pallas_call x1, Pallas kernels, rest_grads(): pl.pallas_call(rest_grads_kernel, grid=(steps,), out_shape=[sds((num_head...  14.7 us
    pallas_call x1, Pallas kernels, mlp_grads(): pl.pallas_call(mlp_grads_kernel, grid=(steps,), out_shape=[sds((dim, ffn)...  13.9 us
    pallas_call x1, Pallas kernels, lookup(): pl.pallas_call(lookup_kernel, out_shape=[sds((CORES, CHIPS, seq // (CHIPS...  10.9 us

profile of v1, /device:TPU:113, one launch (start us, length us, event | category | flops | bytes accessed | tf_op | source)
XLA Modules:
  0.0 143.7 jit_solution(16943358617427449218)
XLA Ops:
  0.6 10.9 %lookup.1 = (bf16[2,4,16,3072]{3,2,1,0:T(8,128)(2,1)}, f32[128,128]{1,0:T(8,128)}, f32[128,128]{1,0:T(8,128)}) custom-call(s32[1,128]{1,0:T(1,128)} %tokens.1, s32[1,128]{1,0:T(1,128)} %tokens.1, s32[1,128]{1,0:T(1,128)} %pos_ref.1, f32[128,1]{1,0:T(8,128)} %constant.2.clone.freq_ref, bf16[2048,3072]{1,0:T(8,128)(2,1)} %emb_hbm.1), custom_call_target="tpu_custom_call" | custom-call | tf_op jit(solution)/shard_map/lookup/pallas_call | solution.py:245
  11.5 103.5 %layer.1 = (bf16[16,3072]{1,0:T(8,128)(2,1)}, f32[2,3072]{1,0:T(2,128)}, bf16[8,16,3072]{2,1,0:T(8,128)(2,1)}, bf16[8,16,3072]{2,1,0:T(8,128)(2,1)}, bf16[8,16,3...) custom-call(bf16[2,4,16,3072]{3,2,1,0:T(8,128)(2,1)} %get-tuple-elem, ...), custom_call_target="tpu_custom_call" | custom-call | tf_op jit(solution)/shard_map/layer/pallas_call | solution.py:490
  115.1 14.7 %rest_grads.1 = (f32[3,3072,128]{2,1,0:T(8,128)}, f32[3072,128]{1,0:T(8,128)}, f32[3072,128]{1,0:T(8,128)}, f32[384,3072]{1,0:T(8,128)}, f32[2048,3072]{1,0:T(8,...) custom-call(bf16[128,3072]{1,0:T(8,128)(2,1)} %bitcast.27, ...), custom_call_target="tpu_custom_call" | custom-call | tf_op jit(solution)/shard_map/rest_grads/pallas_call | solution.py:556
  129.8 13.9 %mlp_grads.1 = (f32[3072,1024]{1,0:T(8,128)}, f32[3072,1024]{1,0:T(8,128)}, f32[1024,3072]{1,0:T(8,128)}) custom-call(bf16[128,3072]{1,0:T(8,128)(2,1)} %bitcast.25, bf16[128,1024]{1,0:T(8,128)(2,1)} %get-tuple-element.54.dgate, bf16[128,1024]{1,0:T(8,128)(2,1)} %get-tuple-element.55.dup, bf16[128,1024]{1,0:T(8,128)(2,1)} %get-tuple-element.56.act, ...), custom_call_target="tpu_custom_call" | custom-call | tf_op jit(solution)/shard_map/mlp_grads/pallas_call | solution.py:509
